TPU v7x, 32 devices: a whole 2x2x4 slice. The times are simulated.
32 devices in a mesh: groups: 2 (over x), row: 8 (over z, y), head: 2 (over core).
Axes of the slice: x: 2, y: 2, z: 4, core: 2. Of those that a mesh axis runs over, the one named last changes fastest.
Arguments:
- hidden: bfloat16 [48, 4096], P('groups'), parts along dimension 0, may hold values from -6 to 6
- norm_gain: float32 [4096], replicated, may hold values from 0.1 to 1.9
- w_query: bfloat16 [8, 256, 4096], P('head', 'row'), may hold values from -0.09375 to 0.09375
- w_key: bfloat16 [8, 256, 4096], P('head', 'row'), may hold values from -0.09375 to 0.09375
- w_value: bfloat16 [8, 512, 4096], P('head', 'row'), may hold values from -0.09375 to 0.09375
- w_outgate: bfloat16 [8, 512, 4096], P('head', 'row'), may hold values from -0.09375 to 0.09375
- w_out: bfloat16 [8, 512, 4096], P('head', 'row'), may hold values from -0.125 to 0.125
- w_gates: bfloat16 [2, 8, 4096], P(None, 'head'), may hold values from -0.09375 to 0.09375
- gate_bias: float32 [2, 8], P(None, 'head'), may hold values from -2 to 4
- headnorm_gain: float32 [8, 512], P('head', 'row'), may hold values from 0.1 to 1.9
- final_gain: float32 [4096], replicated, may hold values from 0.1 to 1.9
- w_vocab: bfloat16 [25152, 4096], P(('row', 'head')), may hold values from -39.0625 to 39.0625
- memory: float32 [48, 8, 256, 512], P('groups', 'head', 'row'), parts along dimension 0, may hold values from -6 to 6
- normalizer: float32 [48, 8, 256], P('groups', 'head', 'row'), parts along dimension 0, may hold values from -6 to 6
- stabilizer: float32 [48, 8], P('groups', 'head'), parts along dimension 0, may hold values from -2 to 2
- targets: int32 [48], P('groups'), parts along dimension 0, may hold values from 0 to 25151
Outputs:
- memory_out: float32 [48, 8, 256, 512], P('groups', 'head', 'row'), parts along dimension 0
- normalizer_out: float32 [48, 8, 256], P('groups', 'head', 'row'), parts along dimension 0
- stabilizer_out: float32 [48, 8], P('groups', 'head'), parts along dimension 0
- hidden_out: bfloat16 [48, 4096], P('groups', ('row', 'head')), parts along dimension 0
- log_prob: float32 [48], P('groups'), parts along dimension 0
There are 2 independent parts, one for each index of `groups`. A program takes and returns all parts, laid end to end along the dimension named above; an argument that names none is the same for every part. Nothing has to cross between parts.
All inputs are finite; a program needn't handle non-finite values.
Results may differ from a plain program's by a relative error of at most 0.0035.
The roundings to bfloat16 on the way count: a program that leaves them out, or rounds other values in their place, can miss the bound.
Values may be sent and summed in bfloat16 or wider, within the bound.
A program may use at most 64 MiB of HBM per device.

v0:
```python
import math
import jax
import jax.numpy as jnp
from jax import lax
from jax.sharding import PartitionSpec as P

QK_DIM = 256
epsilon = 1e-06


def joined_2(value, axis, join):
    pieces = jax.tree.map(lambda part: lax.all_gather(part, axis), value)
    head = jax.tree.map(lambda part: part[0], pieces)
    tail = jax.tree.map(lambda part: part[1:], pieces)
    total, _ = lax.scan(lambda total, share: (join(total, share), None), head, tail)
    return total


def rms_round(stream, gain):
    scale = lax.rsqrt(jnp.mean(stream * stream, axis=-1, keepdims=True) + epsilon)
    return (stream * scale * gain).astype(jnp.bfloat16)


def per_device(
    hidden,
    norm_gain,
    w_query,
    w_key,
    w_value,
    w_outgate,
    w_out,
    w_gates,
    gate_bias,
    headnorm_gain,
    final_gain,
    w_vocab,
    memory,
    normalizer,
    stabilizer,
    targets,
):
    value_rows = w_value.shape[1]
    stream = hidden.astype(jnp.float32)
    normed_in = rms_round(stream, norm_gain)

    def project(weights):
        return jnp.einsum("sd,hjd->shj", normed_in, weights, preferred_element_type=jnp.float32)

    queries = project(w_query) / math.sqrt(QK_DIM)
    key_part = project(w_key)
    value_part = project(w_value).astype(jnp.bfloat16)
    outgate_pre = project(w_outgate)
    gate_pre = (
        jnp.einsum("sd,ghd->gsh", normed_in, w_gates, preferred_element_type=jnp.float32)
        + gate_bias[:, None, :]
    )
    log_forget = jax.nn.log_sigmoid(gate_pre[1])
    stabilizer_out = jnp.maximum(log_forget + stabilizer, gate_pre[0])
    decay_rate = jnp.exp(log_forget + stabilizer - stabilizer_out)
    inflow = jnp.exp(gate_pre[0] - stabilizer_out)
    scaled_key = inflow[:, :, None] * key_part
    memory_out = (
        decay_rate[:, :, None, None] * memory
        + scaled_key[:, :, :, None]
        * lax.all_gather(value_part, "row", axis=2, tiled=True).astype(jnp.float32)[:, :, None, :]
    )
    normalizer_out = decay_rate[:, :, None] * normalizer + scaled_key
    partial_readout = jnp.einsum(
        "shj,shje->she", queries, memory_out, precision=lax.Precision.HIGHEST
    )
    readout = lax.psum(partial_readout, "row")
    average = jnp.mean(readout, axis=-1)
    centered_full = readout - average[:, :, None]
    variance = jnp.mean(centered_full * centered_full, axis=-1)
    centered = lax.dynamic_slice_in_dim(
        centered_full, lax.axis_index("row") * value_rows, value_rows, 2
    )
    normed = centered * lax.rsqrt(variance + epsilon)[:, :, None] * headnorm_gain
    gated_out = (jax.nn.sigmoid(outgate_pre) * normed).astype(jnp.bfloat16)
    partial_terms = jnp.einsum("shj,hjd->sd", gated_out, w_out, preferred_element_type=jnp.float32)
    position = lax.axis_index("row") * lax.axis_size("head") + lax.axis_index("head")
    share_width = hidden.shape[1] // (lax.axis_size("row") * lax.axis_size("head"))
    vocab_here = w_vocab.shape[0]
    projection = lax.psum(partial_terms, ("row", "head"))
    new_full = (stream + projection).astype(jnp.bfloat16)
    final_feat = rms_round(new_full.astype(jnp.float32), final_gain)
    logits = jnp.einsum("sd,vd->sv", final_feat, w_vocab, preferred_element_type=jnp.float32)
    hidden_out = lax.dynamic_slice_in_dim(new_full, position * share_width, share_width, 1)
    local_ids = targets - position * vocab_here
    is_target = jnp.arange(vocab_here, dtype=jnp.int32)[None, :] == local_ids[:, None]
    target_term = jnp.sum(jnp.where(is_target, logits, 0.0), axis=-1)
    local_max = jnp.max(logits, axis=-1)
    local_sum = jnp.sum(jnp.exp(logits - local_max[:, None]), axis=-1)

    def combine(earlier, later):
        highest = jnp.maximum(earlier[0], later[0])
        joined = earlier[1] * jnp.exp(earlier[0] - highest) + later[1] * jnp.exp(later[0] - highest)
        return (highest, joined, earlier[2] + later[2])

    highest, exp_total, picked = joined_2(
        (local_max, local_sum, target_term), ("row", "head"), combine
    )
    log_prob = picked - (highest + jnp.log(exp_total))
    return (memory_out, normalizer_out, stabilizer_out, hidden_out, log_prob)


def solution(mesh):
    in_specs = (
        P("groups", None),
        P(),
        P("head", "row", None),
        P("head", "row", None),
        P("head", "row", None),
        P("head", "row", None),
        P("head", "row", None),
        P(None, "head", None),
        P(None, "head"),
        P("head", "row"),
        P(),
        P(("row", "head"), None),
        P("groups", "head", "row", None),
        P("groups", "head", "row"),
        P("groups", "head"),
        P("groups"),
    )
    out_specs = (
        P("groups", "head", "row", None),
        P("groups", "head", "row"),
        P("groups", "head"),
        P("groups", ("row", "head")),
        P("groups"),
    )
    return jax.shard_map(
        per_device, mesh=mesh, in_specs=in_specs, out_specs=out_specs, check_vma=False
    )
```

profile of v0, /device:TPU:0, one launch (start us, length us, event | category | flops | bytes accessed | tf_op | source)
XLA Modules:
  0.0 280.0 jit_solution(1592682969917463788)
XLA Ops:
  7.2 0.0 copy-start
  7.2 0.0 all-reduce.7.cloned.1.call-start
  7.2 1.2 fusion.17
  8.5 2.7 convolution_convert_fusion
  11.1 0.1 copy.34
  11.3 33.0 %all_gather.21 = bf16[24,4,512]{0,1,2:T(4,128)(2,1)S(1)} all-gather(bf16[24,4,64]{0,1,2:T(4,128)(2,1)S(1)} %copy.34), channel_id=1, replica_groups=mesh['groups'=2,'row'=8,'head'=2] {'row'}, dimensions={2}, use_global_device_ids=true | all-gather | bytes 110592 | tf_op jit(solution)/shard_map/all_gather | solution.py:65
  44.3 0.3 copy.35
  44.6 0.1 copy.36
  44.7 1.2 fusion.13
  45.9 0.7 subtract_exponential_fusion.1
  46.6 0.0 copy-start.5
  46.6 0.1 copy.32
  46.7 2.2 fusion.28
  48.9 2.2 fusion.7
  51.1 3.4 %multiply_add_fusion = f32[24,4,32,512]{3,2,1,0:T(8,128)S(1)} fusion(f32[24,4,32,512]{3,2,1,0:T(8,128)} %param.30, f32[24,4,512]{2,1,0:T(4,128)S(1)} %copy.36, f32[24,4,32]{2,1,0:T(4,128)S(1)} %copy.33, f32[24,4]{1,0:T(8,128)S(1)} %copy.32), kind=kLoop, calls=%fused_computation.10 | loop fusion | flops 4718592 | bytes 12792192 | tf_op jit(solution)/shard_map/add | solution.py:63
  54.5 0.0 copy-start.1
  54.5 2.7 copy-done.1
  57.2 0.0 copy-start.7
  57.2 0.0 copy-start.4
  57.2 3.1 %fusion.26 = f32[24,4,1,512]{3,2,1,0:T(1,128)S(1)} fusion(f32[24,4,32,512]{3,2,1,0:T(8,128)S(1)} %multiply_add_fusion, f32[24,4,32,1]{2,0,1,3:T(8,128)S(1)} %fusion.7), kind=kOutput, calls=%fused_computation.46 | convolution fusion | flops 18874368 | bytes 6500352 | tf_op jit(solution)/shard_map/shj,shje->she/dot_general | solution.py:68
  60.4 0.7 copy.47
  61.1 0.0 all-reduce.7.cloned.1.call-update
  61.1 0.0 all-reduce.9.cloned.1.call-start
  61.2 0.6 copy.38
  61.8 0.6 dynamic-slice
  63.1 70.0 %all-reduce.7.cloned.1.call-done = f32[24,4,512]{2,0,1:T(8,128)} async-done(((f32[24,4,512]{2,0,1:T(8,128)}), f32[24,4,512]{2,0,1:T(8,128)}) %all-reduce.7.cloned.1.call-update) | async-done | bytes 196624 | tf_op jit(solution)/shard_map/psum | solution.py:71
  133.1 1.0 reduce_sum.55
  134.1 1.1 multiply_reduce_fusion
  135.3 3.8 %convolution_bitcast_fusion = f32[24,4096]{1,0:T(8,128)} fusion(bf16[4,64,4096]{2,1,0:T(8,128)(2,1)S(1)} %copy-done, bf16[4,64,4096]{2,1,0:T(8,128)(2,1)} %param.23, f32[24,4,512]{2,0,1:T(8,128)S(1)} %get-tuple-element.86, s32[]{:T(128)S(6)} %select_n.16, f32[4,64]{1,0:T(4,128)S(1)} %copy-done.6, f32[24,4]{0,1:T(4,128)S(1)} %add_rsqrt_fusion, ...), kind=kOutput, calls=%fused_computation.11 | convolution fusion | flops 101099520 | bytes 4854276 | tf_op jit(solution)/shard_map/shj,hjd->sd/dot_general | solution.py:80
  139.0 0.0 all-reduce.9.cloned.1.call-update
  139.1 90.6 %all-reduce.9.cloned.1.call-done = f32[24,4096]{1,0:T(8,128)} async-done(((f32[24,4096]{1,0:T(8,128)}), f32[24,4096]{1,0:T(8,128)}) %all-reduce.9.cloned.1.call-update) | async-done | bytes 393232 | tf_op jit(solution)/shard_map/psum | solution.py:84
  229.6 1.2 fusion.14
  230.8 0.0 copy-done.4
  230.8 8.3 %fusion.50 = (f32[24]{0:T(128)S(1)}, f32[24,1572]{1,0:T(8,128)S(1)}) fusion(bf16[1572,4096]{1,0:T(8,128)(2,1)} %param.29, bf16[24,4096]{1,0:T(8,128)(2,1)S(1)} %get-tuple-element.84, f32[4096]{0:T(1024)S(1)} %copy-done.4, f32[24]{0:T(128)S(1)} %add_rsqrt_fusion.1), kind=kOutput, calls=%fused_computation.74 | convolution fusion | flops 309498688 | bytes 13241920 | tf_op jit(solution)/shard_map/sd,vd->sv/dot_general | solution.py:87
  239.1 0.2 dynamic-update-slice
  239.3 0.2 select_reduce_fusion
  239.6 0.2 dynamic-update-slice.1
  239.8 0.2 dynamic-update-slice.2
  240.0 30.9 %all-reduce.3 = (f32[384]{0:T(512)S(1)}, f32[384]{0:T(512)S(1)}, f32[384]{0:T(512)S(1)}) all-reduce(f32[384]{0:T(512)S(1)} %dynamic-update-slice, f32[384]{0:T(512)S(1)} %dynamic-update-slice.1, f32[384]{0:T(512)S(1)} %dynamic-update-slice.2), channel_id=2, replica_groups=mesh['groups'=2,'row'=8,'head'=2] {'row','head'}, use_global_device_ids=true, to_apply=%add | all-reduce | flops 1152 | bytes 9216
  271.0 0.1 slice.36
  271.0 0.1 slice.37
  271.1 0.1 slice.38
  271.2 0.6 constant_dynamic-slice_fusion.3
  271.8 0.1 reshape.55
  271.9 0.1 reshape.56
  271.9 0.1 reshape.57
  272.0 0.6 while.14
  272.7 0.5 add_subtract_fusion
  (39 shorter events, 0.5 us)
Async XLA Ops:
  7.2 128.1 %copy-start = (bf16[4,64,4096]{2,1,0:T(8,128)(2,1)S(1)}, bf16[4,64,4096]{2,1,0:T(8,128)(2,1)}, u32[]{:S(2)}) copy-start(bf16[4,64,4096]{2,1,0:T(8,128)(2,1)} %param.24) | copy-start | bytes 6291460
  7.2 125.9 %all-reduce.7.cloned.1.call-start = ((), (), s32[]{:S(2)}) async-start(), calls=%async_computation | async-start | bytes 393216 | tf_op jit(solution)/shard_map/psum | solution.py:71
  46.6 7.9 %copy-start.5 = (f32[24,4]{0,1:T(4,128)}, f32[24,4]{0,1:T(4,128)S(1)}, u32[]{:S(2)}) copy-start(f32[24,4]{0,1:T(4,128)S(1)} %get-tuple-element.88) | copy-start | bytes 1156
  54.5 2.7 copy-start.1
  57.2 4.6 %copy-start.8 = (u32[32]{0:T(128)S(1)}, u32[32]{0:T(128)}, u32[]{:S(2)}) copy-start(u32[32]{0:T(128)} %constant.57) | copy-start | bytes 388
  57.2 78.0 %copy-start.2 = (bf16[24,4096]{1,0:T(8,128)(2,1)S(1)}, bf16[24,4096]{1,0:T(8,128)(2,1)}, u32[]{:S(2)}) copy-start(bf16[24,4096]{1,0:T(8,128)(2,1)} %param.18) | copy-start | bytes 589828
  57.2 78.0 %copy-start.3 = (f32[4096]{0:T(1024)S(1)}, f32[4096]{0:T(1024)}, u32[]{:S(2)}) copy-start(f32[4096]{0:T(1024)} %param.19) | copy-start | bytes 49156
  57.2 78.1 %copy-start.6 = (f32[4,64]{1,0:T(4,128)S(1)}, f32[4,64]{1,0:T(4,128)}, u32[]{:S(2)}) copy-start(f32[4,64]{1,0:T(4,128)} %param.27) | copy-start | bytes 3076
  57.2 81.8 %copy-start.7 = (s32[24]{0:T(128)S(1)}, s32[24]{0:T(128)}, u32[]{:S(2)}) copy-start(s32[24]{0:T(128)} %param.33) | copy-start | bytes 292
  57.2 173.6 %copy-start.4 = (f32[4096]{0:T(1024)S(1)}, f32[4096]{0:T(1024)}, u32[]{:S(2)}) copy-start(f32[4096]{0:T(1024)} %param.28) | copy-start | bytes 49156
  61.1 168.5 %all-reduce.9.cloned.1.call-start = ((), (), s32[]{:S(2)}) async-start(), calls=%async_computation.1 | async-start | bytes 786432 | tf_op jit(solution)/shard_map/psum | solution.py:84
Sparse Core Ops, SparseCore 0:
  61.2 71.7 all-reduce.6
  139.2 90.4 all-reduce.8
where the time goes:
time: 281 us; the launch traced here: 280 us
  waiting for transfers between devices  161 us (57%)
  blocking collectives  64 us (23%)
  matrix products  23.4 us (8%)
  between operations  15 us (5%)
  other arithmetic  9.78 us (3%)
  local copies, waits for them, and re-layouts  7.02 us (2%)
    psum x1, waiting for transfers between devices, per_device(): projection = lax.psum(partial_terms, ('row', 'head'))  90.6 us
    psum x1, waiting for transfers between devices, per_device(): readout = lax.psum(partial_readout, 'row')  70 us
    all_gather x1, blocking collectives, per_device(): lax.all_gather(value_part, 'row', axis=2, tiled=True).astype(jnp.float32)  33 us
    unnamed x1, blocking collectives  30.9 us
    dot_general x1, matrix products, per_device(): jnp.einsum('sd,vd->sv', final_feat, w_vocab, preferred_element_type=jnp.f...  8.26 us
    dot_general x3, matrix products, project(): jnp.einsum('sd,hjd->shj', normed_in, weights, preferred_element_type=jnp....  7.03 us
  transfers between devices with their start and end apart: 2, of which 2 were waited for; matrix products, arithmetic and copies ran while one was open for 0% of the time, Pallas kernels for 0%

commit v1 on v0

--- a/solution.py
+++ b/solution.py
@@ -68,7 +68,9 @@
     partial_readout = jnp.einsum(
         "shj,shje->she", queries, memory_out, precision=lax.Precision.HIGHEST
     )
-    readout = lax.psum(partial_readout, "row")
+    readout = partial_readout
+    for hop in (1, 2, 4):
+        readout = readout + lax.ppermute(readout, "row", [(dev, dev ^ hop) for dev in range(8)])
     average = jnp.mean(readout, axis=-1)
     centered_full = readout - average[:, :, None]
     variance = jnp.mean(centered_full * centered_full, axis=-1)

time: 281 us -> 229 us (0.81)
  waiting for transfers between devices: 161 us -> 109 us
    psum x1 -> x0, waiting for transfers between devices: 70 us -> none  [per_device(): readout = lax.psum(partial_readout, 'row')]
    ppermute x0 -> x3, waiting for transfers between devices: none -> 17.4 us  [per_device(): lax.ppermute(readout, 'row', [(dev, dev ^ hop) for dev in range(8)])]
  transfers between devices with their start and end apart: 2 -> 4, of which waited for: 2 -> 4; matrix products, arithmetic and copies ran while one was open for 0% -> 1% of each run, Pallas kernels for 0% -> 0%
where the time goes in v1:
time: 229 us; the launch traced here: 228 us
  waiting for transfers between devices  109 us (48%)
  blocking collectives  64 us (28%)
  matrix products  23.4 us (10%)
  between operations  15 us (7%)
  other arithmetic  8.06 us (4%)
  local copies, waits for them, and re-layouts  6.35 us (3%)
  starting transfers between devices  2.46 us (1%)
    psum x1, waiting for transfers between devices, per_device(): projection = lax.psum(partial_terms, ('row', 'head'))  91.4 us
    all_gather x1, blocking collectives, per_device(): lax.all_gather(value_part, 'row', axis=2, tiled=True).astype(jnp.float32)  33 us
    unnamed x1, blocking collectives  30.9 us
    ppermute x3, waiting for transfers between devices, per_device(): lax.ppermute(readout, 'row', [(dev, dev ^ hop) for dev in range(8)])  17.4 us
    dot_general x1, matrix products, per_device(): jnp.einsum('sd,vd->sv', final_feat, w_vocab, preferred_element_type=jnp.f...  8.26 us
    dot_general x3, matrix products, project(): jnp.einsum('sd,hjd->shj', normed_in, weights, preferred_element_type=jnp....  7.03 us
    unnamed x26, local copies, waits for them, and re-layouts  4.65 us
  transfers between devices with their start and end apart: 4, of which 4 were waited for; matrix products, arithmetic and copies ran while one was open for 1% of the time, Pallas kernels for 0%

profile of v1, /device:TPU:0, one launch (start us, length us, event | category | flops | bytes accessed | tf_op | source)
XLA Modules:
  0.0 228.2 jit_solution(13275114867615843353)
XLA Ops:
  7.2 0.0 copy-start
  7.2 0.0 all-reduce.6.cloned.1.call-start
  7.2 1.2 fusion.15
  8.5 2.7 %convolution_convert_fusion = bf16[24,4,64]{2,0,1:T(8,128)(2,1)S(1)} fusion(bf16[4,64,4096]{2,1,0:T(8,128)(2,1)} %param.22, bf16[24,4096]{1,0:T(8,128)(2,1)} %param.18, f32[4096]{0:T(1024)} %param.19, f32[24]{0:T(128)S(1)} %add_rsqrt_fusion.2), kind=kOutput, calls=%fused_computation.19 | convolution fusion | flops 50731008 | bytes 2322528 | tf_op jit(solution)/shard_map/sd,hjd->shj/dot_general | solution.py:47
  11.1 0.1 copy.34
  11.3 33.0 %all_gather.21 = bf16[24,4,512]{0,1,2:T(4,128)(2,1)S(1)} all-gather(bf16[24,4,64]{0,1,2:T(4,128)(2,1)S(1)} %copy.34), channel_id=1, replica_groups=mesh['groups'=2,'row'=8,'head'=2] {'row'}, dimensions={2}, use_global_device_ids=true | all-gather | bytes 110592 | tf_op jit(solution)/shard_map/all_gather | solution.py:65
  44.3 0.3 copy.35
  44.6 0.1 copy.36
  44.7 1.2 fusion.11
  45.9 0.7 subtract_exponential_fusion.1
  46.6 0.1 copy.32
  46.7 2.2 fusion.26
  48.9 2.2 fusion.7
  51.1 3.4 %multiply_add_fusion = f32[24,4,32,512]{3,2,1,0:T(8,128)S(1)} fusion(f32[24,4,32,512]{3,2,1,0:T(8,128)} %param.30, f32[24,4,512]{2,1,0:T(4,128)S(1)} %copy.36, f32[24,4,32]{2,1,0:T(4,128)S(1)} %copy.33, f32[24,4]{1,0:T(8,128)S(1)} %copy.32), kind=kLoop, calls=%fused_computation.10 | loop fusion | flops 4718592 | bytes 12792192 | tf_op jit(solution)/shard_map/add | solution.py:63
  54.5 0.0 copy-start.1
  54.5 2.7 %copy-done.1 = f32[24,4,32,512]{3,2,1,0:T(8,128)} copy-done((f32[24,4,32,512]{3,2,1,0:T(8,128)}, f32[24,4,32,512]{3,2,1,0:T(8,128)S(1)}, u32[]{:S(2)}) %copy-start.1) | copy-done | bytes 6291480
  57.2 3.1 %fusion.24 = f32[24,4,1,512]{3,2,1,0:T(1,128)S(1)} fusion(f32[24,4,32,512]{3,2,1,0:T(8,128)S(1)} %multiply_add_fusion, f32[24,4,32,1]{2,0,1,3:T(8,128)S(1)} %fusion.7), kind=kOutput, calls=%fused_computation.44 | convolution fusion | flops 18874368 | bytes 6500352 | tf_op jit(solution)/shard_map/shj,shje->she/dot_general | solution.py:68
  60.4 0.1 copy.49
  60.4 1.8 collective-permute-start
  62.2 3.9 %collective-permute-done = f32[24,4,512]{2,0,1:T(8,128)S(1)} collective-permute-done((f32[24,4,512]{2,0,1:T(8,128)S(1)}, f32[24,4,512]{2,0,1:T(8,128)S(1)}, u32[]{:S(2)}, u32[]{:S(2)}) %collective-permute-start) | collective-permute-done | bytes 196640 | tf_op jit(solution)/shard_map/ppermute | solution.py:73
  66.2 0.1 fusion.36
  66.3 0.1 collective-permute-start.1
  66.3 7.7 %collective-permute-done.1 = f32[24,4,512]{2,0,1:T(8,128)S(1)} collective-permute-done((f32[24,4,512]{2,0,1:T(8,128)S(1)}, f32[24,4,512]{2,0,1:T(8,128)S(1)}, u32[]{:S(2)}, u32[]{:S(2)}) %collective-permute-start.1) | collective-permute-done | bytes 196640 | tf_op jit(solution)/shard_map/ppermute | solution.py:73
  74.0 0.6 collective-permute-start.2
  74.6 0.6 copy.38
  75.2 0.6 dynamic-slice
  76.5 5.8 %collective-permute-done.2 = f32[24,4,512]{2,0,1:T(8,128)S(1)} collective-permute-done((f32[24,4,512]{2,0,1:T(8,128)S(1)}, f32[24,4,512]{2,0,1:T(8,128)S(1)}, u32[]{:S(2)}, u32[]{:S(2)}) %collective-permute-start.2) | collective-permute-done | bytes 196640 | tf_op jit(solution)/shard_map/ppermute | solution.py:73
  82.3 0.1 fusion.45
  82.4 0.2 multiply_reduce_fusion
  82.6 3.8 %convolution_bitcast_fusion = f32[24,4096]{1,0:T(8,128)} fusion(bf16[4,64,4096]{2,1,0:T(8,128)(2,1)S(1)} %copy-done, f32[24,4,512]{2,0,1:T(8,128)S(1)} %get-tuple-element.86, s32[]{:T(128)S(6)} %select_n.16, bf16[4,64,4096]{2,1,0:T(8,128)(2,1)} %param.23, f32[4,64]{1,0:T(4,128)S(1)} %copy-done.6, f32[24,4]{0,1:T(4,128)S(1)} %add_rsqrt_fusion, ...), kind=kOutput, calls=%fused_computation.11 | convolution fusion | flops 101099520 | bytes 4854276 | tf_op jit(solution)/shard_map/shj,hjd->sd/dot_general | solution.py:82
  86.4 0.0 all-reduce.6.cloned.1.call-update
  86.4 91.4 %all-reduce.6.cloned.1.call-done = f32[24,4096]{1,0:T(8,128)} async-done(((f32[24,4096]{1,0:T(8,128)}), f32[24,4096]{1,0:T(8,128)}) %all-reduce.6.cloned.1.call-update) | async-done | bytes 393232 | tf_op jit(solution)/shard_map/psum | solution.py:86
  177.8 1.2 fusion.12
  179.0 8.3 %fusion.47 = (f32[24]{0:T(128)S(1)}, f32[24,1572]{1,0:T(8,128)S(1)}) fusion(bf16[1572,4096]{1,0:T(8,128)(2,1)} %param.29, bf16[24,4096]{1,0:T(8,128)(2,1)S(1)} %get-tuple-element.84, f32[4096]{0:T(1024)S(1)} %copy-done.4, f32[24]{0:T(128)S(1)} %add_rsqrt_fusion.1), kind=kOutput, calls=%fused_computation.72 | convolution fusion | flops 309498688 | bytes 13241920 | tf_op jit(solution)/shard_map/sd,vd->sv/dot_general | solution.py:89
  187.3 0.2 dynamic-update-slice
  187.5 0.2 select_reduce_fusion
  187.7 0.2 dynamic-update-slice.1
  188.0 0.2 dynamic-update-slice.2
  188.2 30.9 %all-reduce.3 = (f32[384]{0:T(512)S(1)}, f32[384]{0:T(512)S(1)}, f32[384]{0:T(512)S(1)}) all-reduce(f32[384]{0:T(512)S(1)} %dynamic-update-slice, f32[384]{0:T(512)S(1)} %dynamic-update-slice.1, f32[384]{0:T(512)S(1)} %dynamic-update-slice.2), channel_id=2, replica_groups=mesh['groups'=2,'row'=8,'head'=2] {'row','head'}, use_global_device_ids=true, to_apply=%add | all-reduce | flops 1152 | bytes 9216
  219.1 0.1 slice.36
  219.2 0.1 slice.37
  219.3 0.1 slice.38
  219.4 0.6 constant_dynamic-slice_fusion.3
  220.0 0.1 reshape.55
  220.0 0.1 reshape.56
  220.1 0.1 reshape.57
  220.2 0.6 while.14
  220.9 0.5 add_subtract_fusion
  (44 shorter events, 0.6 us)
Async XLA Ops:
  7.2 75.4 %copy-start = (bf16[4,64,4096]{2,1,0:T(8,128)(2,1)S(1)}, bf16[4,64,4096]{2,1,0:T(8,128)(2,1)}, u32[]{:S(2)}) copy-start(bf16[4,64,4096]{2,1,0:T(8,128)(2,1)} %param.24) | copy-start | bytes 6291460
  7.2 170.6 %all-reduce.6.cloned.1.call-start = ((), (), s32[]{:S(2)}) async-start(), calls=%async_computation | async-start | bytes 786432 | tf_op jit(solution)/shard_map/psum | solution.py:86
  46.6 7.9 %copy-start.5 = (f32[24,4]{0,1:T(4,128)}, f32[24,4]{0,1:T(4,128)S(1)}, u32[]{:S(2)}) copy-start(f32[24,4]{0,1:T(4,128)S(1)} %get-tuple-element.90) | copy-start | bytes 1156
  54.5 2.7 %copy-start.1 = (f32[24,4,32,512]{3,2,1,0:T(8,128)}, f32[24,4,32,512]{3,2,1,0:T(8,128)S(1)}, u32[]{:S(2)}) copy-start(f32[24,4,32,512]{3,2,1,0:T(8,128)S(1)} %multiply_add_fusion) | copy-start | bytes 18874372
  57.2 18.0 %copy-start.8 = (u32[32]{0:T(128)S(1)}, u32[32]{0:T(128)}, u32[]{:S(2)}) copy-start(u32[32]{0:T(128)} %constant.57) | copy-start | bytes 388
  57.2 25.4 %copy-start.2 = (bf16[24,4096]{1,0:T(8,128)(2,1)S(1)}, bf16[24,4096]{1,0:T(8,128)(2,1)}, u32[]{:S(2)}) copy-start(bf16[24,4096]{1,0:T(8,128)(2,1)} %param.18) | copy-start | bytes 589828
  57.2 25.4 %copy-start.3 = (f32[4096]{0:T(1024)S(1)}, f32[4096]{0:T(1024)}, u32[]{:S(2)}) copy-start(f32[4096]{0:T(1024)} %param.19) | copy-start | bytes 49156
  57.2 25.4 %copy-start.6 = (f32[4,64]{1,0:T(4,128)S(1)}, f32[4,64]{1,0:T(4,128)}, u32[]{:S(2)}) copy-start(f32[4,64]{1,0:T(4,128)} %param.27) | copy-start | bytes 3076
  57.2 29.2 %copy-start.7 = (s32[24]{0:T(128)S(1)}, s32[24]{0:T(128)}, u32[]{:S(2)}) copy-start(s32[24]{0:T(128)} %param.33) | copy-start | bytes 292
  57.2 121.8 %copy-start.4 = (f32[4096]{0:T(1024)S(1)}, f32[4096]{0:T(1024)}, u32[]{:S(2)}) copy-start(f32[4096]{0:T(1024)} %param.28) | copy-start | bytes 49156
  60.4 5.7 %collective-permute-start = (f32[24,4,512]{2,0,1:T(8,128)S(1)}, f32[24,4,512]{2,0,1:T(8,128)S(1)}, u32[]{:S(2)}, u32[]{:S(2)}) collective-permute-start(f32[24,4,512]{2,0,1:T(8,128)S(1)} %bitcast.65), channel_id=1, source_target_pairs={{0,2},{2,0},{4,6},{6,4},{8,10},{10,8},{12,14},{14,12},{1,3},{3,1},... | collective-permute-start | bytes 589832 | tf_op jit(solution)/shard_map/ppermute | solution.py:73
  66.3 7.7 %collective-permute-start.1 = (f32[24,4,512]{2,0,1:T(8,128)S(1)}, f32[24,4,512]{2,0,1:T(8,128)S(1)}, u32[]{:S(2)}, u32[]{:S(2)}) collective-permute-start(f32[24,4,512]{2,0,1:T(8,128)S(1)} %fusion.36), channel_id=1, source_target_pairs={{0,4},{2,6},{4,0},{6,2},{8,12},{10,14},{12,8},{14,10},{1,5},{3,7},... | collective-permute-start | bytes 589832 | tf_op jit(solution)/shard_map/ppermute | solution.py:73
  74.0 8.2 %collective-permute-start.2 = (f32[24,4,512]{2,0,1:T(8,128)S(1)}, f32[24,4,512]{2,0,1:T(8,128)S(1)}, u32[]{:S(2)}, u32[]{:S(2)}) collective-permute-start(f32[24,4,512]{2,0,1:T(8,128)S(1)} %add.100), channel_id=1, source_target_pairs={{0,8},{2,10},{4,12},{6,14},{8,0},{10,2},{12,4},{14,6},{1,9},{3,11}... | collective-permute-start | bytes 589832 | tf_op jit(solution)/shard_map/ppermute | solution.py:73
Sparse Core Ops, SparseCore 0:
  86.5 91.2 all-reduce.5
